TPU v7x, 32 devices: a whole 2x2x4 slice. The times are simulated.
32 devices in a mesh: dp: 4 (over x, core), ctx: 8 (over z, y).
Axes of the slice: x: 2, y: 2, z: 4, core: 2. Of those that a mesh axis runs over, the one named last changes fastest.
Arguments:
- tokens: bfloat16 [4, 4096, 2048], P('dp', 'ctx'), may hold values from -6 to 6
- in_weight: bfloat16 [2048, 5120], P(None, 'dp'), may hold values from -0.125 to 0.125
- step_weight: bfloat16 [2048, 64], replicated, may hold values from -0.125 to 0.125
- step_bias: float32 [64], replicated, may hold values from -3 to 0
- decay_rate: float32 [64], replicated, may hold values from 0.0001 to 0.5
- skip_gain: float32 [64], replicated, may hold values from 0.5 to 1.5
- filter_taps: float32 [4, 5120], replicated, may hold values from -3 to 3
- filter_bias: float32 [5120], replicated, may hold values from -3 to 3
- norm_gain: float32 [4096], replicated, may hold values from 0.5 to 1.5
Outputs:
- normed: bfloat16 [4, 4096, 4096], P('dp', 'ctx')
All inputs are finite; a program needn't handle non-finite values.
Results may differ from a plain program's by a relative error of at most 0.0061.
Values may be sent and summed in bfloat16 or wider, within the bound.
A program may use at most 192 MiB of HBM per device.

v0:
```python
import math
import jax
import jax.numpy as jnp
from jax import lax
from jax.sharding import PartitionSpec as P

HEADS = 64
HEAD_DIM = 64
STATE = 128
GROUPS = 4
BLOCK = 256
GROUP_HEADS = 16


def shifted(value, axis, steps):
    count = lax.axis_size(axis)
    initial, last = (max(0, -steps), min(count, count - steps))
    return lax.ppermute(value, axis, [(source, source + steps) for source in range(initial, last)])


def filter_rows(prefix, current, filter_taps, filter_bias):
    padded = jnp.concatenate([prefix, current], axis=0).astype(jnp.float32)
    length = current.shape[0]
    summed = filter_bias + filter_taps[0] * padded[0:length]
    for offset in range(1, filter_taps.shape[0]):
        summed = summed + filter_taps[offset] * padded[offset : offset + length]
    return summed


def ssd_group(values, input_map, output_map, step_size, decay_rate, skip_gain, block_len):
    length, head_count, head_width = values.shape
    block_count = length // block_len
    bundle = math.gcd(block_count, 8)
    bundle_count = block_count // bundle
    highest = lax.Precision.HIGHEST
    value_rows = values.reshape(block_count, block_len, head_count, head_width)
    input_rows = input_map.reshape(block_count, block_len, -1)
    output_rows = output_map.reshape(block_count, block_len, -1)
    step_rows = step_size.reshape(block_count, block_len, head_count)
    decay_sum = jnp.cumsum(-step_rows * decay_rate, axis=1)
    causal = (jnp.arange(block_len)[:, None] >= jnp.arange(block_len)[None, :])[None, :, :, None]

    def local_block(pieces):
        value_block, input_block, output_block, step_block, decay_block = pieces
        scores = jnp.einsum(
            "ktn,kun->ktu", output_block, input_block, preferred_element_type=jnp.float32
        )
        decay_gap = jnp.where(causal, decay_block[:, :, None, :] - decay_block[:, None, :, :], 0.0)
        weights = (
            jnp.where(causal, jnp.exp(decay_gap), 0.0)
            * scores[..., None]
            * step_block[:, None, :, :]
        ).astype(jnp.bfloat16)
        within = jnp.einsum(
            "ktuh,kuhp->kthp", weights, value_block, preferred_element_type=jnp.float32
        )
        to_end = jnp.exp(decay_block[:, -1:, :] - decay_block) * step_block
        scaled = (to_end[..., None] * value_block.astype(jnp.float32)).astype(jnp.bfloat16)
        states = jnp.einsum(
            "kuhp,kun->khpn", scaled, input_block, preferred_element_type=jnp.float32
        )
        return (within, states)

    def blocked(array):
        return array.reshape((bundle_count, bundle) + array.shape[1:])

    within, states = lax.map(
        local_block,
        (
            blocked(value_rows),
            blocked(input_rows),
            blocked(output_rows),
            blocked(step_rows),
            blocked(decay_sum),
        ),
    )
    within = within.reshape(block_count, block_len, head_count, head_width)
    states = states.reshape((block_count,) + states.shape[2:])
    totals = decay_sum[:, -1, :]
    running = jnp.cumsum(totals, axis=0)
    starts = running - totals
    before = (jnp.arange(block_count)[:, None] > jnp.arange(block_count)[None, :])[:, :, None]
    mixing = jnp.where(
        before, jnp.exp(jnp.where(before, starts[:, None, :] - running[None, :, :], 0.0)), 0.0
    )
    entering = jnp.einsum("kjh,jhpn->khpn", mixing, states, precision=highest)
    carried = (
        jnp.einsum("khpn,ktn->kthp", entering, output_rows.astype(jnp.float32), precision=highest)
        * jnp.exp(decay_sum)[..., None]
    )
    output = within + carried + skip_gain[:, None] * value_rows.astype(jnp.float32)
    return output.reshape(length, head_count, head_width)


def group_norm(values, norm_gain):
    length = values.shape[0]
    grouped = values.astype(jnp.float32).reshape(length, GROUPS, -1)
    mean_square = jnp.mean(jnp.square(grouped), axis=-1, keepdims=True)
    return (grouped * lax.rsqrt(mean_square + 1e-05)).reshape(length, -1) * norm_gain


def sequence_filter(projected, filter_taps, filter_bias):
    reach_rows = filter_taps.shape[0] - 1
    length = projected.shape[0]
    rim_rows = shifted(projected[length - reach_rows :], "ctx", 1)
    return jax.nn.silu(filter_rows(rim_rows, projected, filter_taps, filter_bias)).astype(
        jnp.bfloat16
    )


def head_layout(source, step_raw, step_bias, decay_rate, skip_gain):
    context_size = lax.axis_size("ctx")
    device = lax.axis_index("ctx")
    length = source.shape[0]
    inner_width = HEADS * HEAD_DIM
    local_heads = HEADS // context_size
    local_width = local_heads * HEAD_DIM
    group_share = max(1, GROUP_HEADS // local_heads)
    local_groups = max(1, local_heads // GROUP_HEADS)
    value_parts = source[:, :inner_width].reshape(length, context_size, local_width)
    map_parts = source[:, inner_width:].reshape(length, 2, GROUPS, STATE)
    map_parts = jnp.repeat(map_parts, group_share, axis=2)
    step_parts = step_raw.reshape(length, context_size, local_heads)
    moved_values, moved_input, moved_output, moved_steps = (
        lax.all_to_all(value_parts, "ctx", split_axis=1, concat_axis=0, tiled=True),
        lax.all_to_all(map_parts[:, 0], "ctx", split_axis=1, concat_axis=0, tiled=True),
        lax.all_to_all(map_parts[:, 1], "ctx", split_axis=1, concat_axis=0, tiled=True),
        lax.all_to_all(step_parts, "ctx", split_axis=1, concat_axis=0, tiled=True),
    )
    full_length = moved_values.shape[0]
    head_values = moved_values.reshape(full_length, local_width)
    input_maps = moved_input.reshape(full_length, local_groups * STATE)
    output_maps = moved_output.reshape(full_length, local_groups * STATE)
    bias_slice = lax.dynamic_slice_in_dim(step_bias, device * local_heads, local_heads, 0)
    rate_slice = lax.dynamic_slice_in_dim(decay_rate, device * local_heads, local_heads, 0)
    skip_slice = lax.dynamic_slice_in_dim(skip_gain, device * local_heads, local_heads, 0)
    step_size = jax.nn.softplus(
        moved_steps.reshape(full_length, local_heads).astype(jnp.float32) + bias_slice
    )
    inputs = head_values.reshape(full_length, local_heads, HEAD_DIM)
    pieces = ssd_group(inputs, input_maps, output_maps, step_size, rate_slice, skip_slice, BLOCK)
    mixed_rows = pieces.reshape(full_length, local_width).astype(jnp.bfloat16)
    return lax.all_to_all(mixed_rows, "ctx", split_axis=0, concat_axis=1, tiled=True)


def per_device(
    tokens,
    in_weight,
    step_weight,
    step_bias,
    decay_rate,
    skip_gain,
    filter_taps,
    filter_bias,
    norm_gain,
):
    token_rows = tokens[0]
    projected = jnp.dot(
        token_rows,
        lax.all_gather(in_weight, "dp", axis=1, tiled=True),
        preferred_element_type=jnp.float32,
    ).astype(jnp.bfloat16)
    step_raw = jnp.dot(token_rows, step_weight, preferred_element_type=jnp.float32).astype(
        jnp.bfloat16
    )
    active = sequence_filter(projected, filter_taps, filter_bias)
    mixed_rows = head_layout(active, step_raw, step_bias, decay_rate, skip_gain)
    return group_norm(mixed_rows, norm_gain).astype(jnp.bfloat16)[None]


def solution(mesh):
    in_specs = (P("dp", "ctx", None), P(None, "dp"), P(), P(), P(), P(), P(), P(), P())
    out_specs = P("dp", "ctx", None)
    return jax.shard_map(
        per_device, mesh=mesh, in_specs=in_specs, out_specs=out_specs, check_vma=False
    )
```

profile of v0, /device:TPU:0, one launch (start us, length us, event | category | flops | bytes accessed | tf_op | source)
XLA Modules:
  0.0 554.3 jit_solution(2078704967498910302)
XLA Ops:
  7.3 0.9 copy-done
  8.1 2.3 fusion.45
  10.5 7.3 %all-to-all-start.1 = ((bf16[512,8,8]{0,2,1:T(8,128)(2,1)}), bf16[512,8,8]{0,2,1:T(8,128)(2,1)S(1)}, u32[]{:S(2)}, u32[]{:S(2)}) async-start(bf16[512,8,8]{0,2,1:T(8,128)(2,1)} %fusion.45), calls=%async_computation.1 | async-start | bytes 131072 | tf_op jit(solution)/shard_map/all_to_all | solution.py:128
  17.8 125.4 %all-gather.2.cloned.1.call-done = bf16[2048,5120]{1,0:T(8,128)(2,1)} async-done(((bf16[2048,1280]{1,0:T(8,128)(2,1)}), bf16[2048,5120]{1,0:T(8,128)(2,1)}) %all-gather.2.cloned.1.call-update) | async-done | bytes 20971536 | tf_op jit(solution)/shard_map/all_gather | solution.py:160
  143.2 15.2 %convolution_convert_fusion = bf16[512,5120]{1,0:T(8,128)(2,1)S(1)} fusion(bf16[2048,5120]{1,0:T(8,128)(2,1)} %all-gather.2.cloned.1.call-done, bf16[1,512,2048]{2,1,0:T(8,128)(2,1)S(1)} %copy-done), kind=kOutput, calls=%fused_computation.49 | convolution fusion | flops 10740039680 | bytes 28311552 | tf_op jit(solution)/shard_map/dot_general | solution.py:158
  158.4 3.4 collective-permute-start
  161.9 1.6 collective-permute-done
  163.5 1.5 maximum_convert_fusion
  165.0 6.7 %multiply_convert_fusion.8 = bf16[512,5120]{1,0:T(8,128)(2,1)S(1)} fusion(f32[515,5120]{1,0:T(8,128)S(1)} %maximum_convert_fusion, f32[5120]{0:T(1024)S(1)} %bitcast.192, f32[5120]{0:T(1024)S(1)} %bitcast.193, f32[5120]{0:T(1024)S(1)} %bitcast.191, f32[5120]{0:T(1024)S(1)} %bitcast.190, f32[5120]{0:T(1024)S(1)} %copy-done.7), kind=kLoop, calls=%fused_computation.40 | loop fusion | flops 34078720 | bytes 47288320 | tf_op jit(solution)/shard_map/convert_element_type | solution.py:106
  171.8 2.3 copy-done.5
  174.1 0.8 reshape.188
  175.5 1.6 slice_bitcast_fusion.1
  177.0 6.4 %all-to-all-start.2 = ((bf16[512,8,128]{2,0,1:T(8,128)(2,1)}), bf16[512,8,128]{2,0,1:T(8,128)(2,1)}, u32[]{:S(2)}, u32[]{:S(2)}) async-start(bf16[512,8,128]{2,0,1:T(8,128)(2,1)} %get-tuple-element.173), calls=%async_computation.2 | async-start | bytes 2097152 | tf_op jit(solution)/shard_map/all_to_all | solution.py:127
  183.4 4.7 slice.75
  188.1 6.5 %copy.167 = bf16[512,4096]{0,1:T(8,128)(2,1)} copy(bf16[512,4096]{1,0:T(8,128)(2,1)} %slice.75) | data formatting | bytes 8388608 | tf_op jit(solution)/shard_map/reshape | solution.py:120
  194.6 14.2 %all-to-all-done.2 = bf16[512,8,128]{2,0,1:T(8,128)(2,1)} async-done(((bf16[512,8,128]{2,0,1:T(8,128)(2,1)}), bf16[512,8,128]{2,0,1:T(8,128)(2,1)}, u32[]{:S(2)}, u32[]{:S(2)}) %all-to-all-start.2) | async-done | bytes 1048608 | tf_op jit(solution)/shard_map/all_to_all | solution.py:127
  208.8 4.6 all-to-all-start
  214.2 91.4 %all-to-all-done = bf16[512,8,512]{0,2,1:T(8,128)(2,1)} async-done(((bf16[512,8,512]{0,2,1:T(8,128)(2,1)}), bf16[512,8,512]{0,2,1:T(8,128)(2,1)}, u32[]{:S(2)}, u32[]{:S(2)}) %all-to-all-start) | async-done | bytes 4194336 | tf_op jit(solution)/shard_map/all_to_all | solution.py:125
  305.6 4.7 all-to-all-start.3
  310.5 9.0 %reduce-window.6 = f32[16,8,2,128]{3,1,2,0:T(8,128)S(1)} reduce-window(f32[16,8,2,128]{3,1,2,0:T(8,128)S(1)} %fusion.50, f32[]{:T(128)} %constant.30.clone.1), window={size=1x1x1x128 pad=0_0x0_0x0_0x127_0}, to_apply=%region_0.1 | reduce-window | flops 4161536 | bytes 262148 | tf_op jit(solution)/shard_map/reduce-window
  321.5 6.5 %copy.143 = bf16[8,512,1,512]{1,0,3,2:T(8,128)(2,1)} copy(bf16[8,512,1,512]{1,3,0,2:T(8,128)(2,1)} %bitcast.7) | data formatting | bytes 8388608 | tf_op jit(solution)/shard_map/all_to_all | solution.py:125
  327.9 7.1 %reshape_reshape_reshape_reshape.3 = bf16[2,8,256,8,64]{2,1,0,4,3:T(8,128)(2,1)} reshape(bf16[8,512,1,512]{1,0,3,2:T(8,128)(2,1)} %copy.143) | data formatting | bytes 8388608 | tf_op jit(solution)/shard_map/reshape;reshape;reshape;reshape | solution.py:65
  335.0 0.9 all-to-all-done.3
  335.9 34.5 %while.14 = (s32[]{:T(128)}, f32[2,8,256,8,64]{2,4,3,1,0:T(8,128)}, f32[2,8,8,64,128]{4,3,2,1,0:T(8,128)}, bf16[2,8,256,8,64]{2,1,0,4,3:T(8,128)(2,1)}, f32[2,8,...) while((s32[]{:T(128)}, f32[2,8,256,8,64]{2,4,3,1,0:T(8,128)}, ...), condition=%wide.region_3.4_spmd.clone.clone, body=%wide.region_2.3_spmd.clone.clone.sunk | while | flops 967933952 | bytes 30084480 | solution.py:67
  335.9 1.6 fusion.77
  337.6 1.7 constant_dynamic-slice_fusion.6
  339.4 1.3 copy-done.2
  340.6 7.4 %bitcast_dynamic-update-slice_fusion.4 = f32[2,8,256,8,64]{2,4,3,1,0:T(8,128)} fusion(f32[2,8,256,8,64]{2,4,3,1,0:T(8,128)} %get-tuple-element.241, s32[]{:T(128)} %get-tuple-element.240, f32[8,256,8]{1,2,0:T(8,128)S(1)} %bitcast.182, f32[8,256,256]{2,1,0:T(8,128)S(1)} %fusion.77, f32[8,256,8]{1,2,0:T(8,128)S(1)} %bitcast.183, ...), kind=kOutput, calls=%fused_computation.9.clone.1 | convolution fusion | flops 562036736 | bytes 8651264 | tf_op jit(solution)/shard_map/while/body/eval_jaxpr/ktuh,kuhp->kthp/dot_general | solution.py:54
  349.4 3.7 bitcast_dynamic-update-slice_fusion.5
  353.1 1.6 fusion.77
  354.8 1.7 constant_dynamic-slice_fusion.6
  356.6 1.3 copy-done.2
  357.9 7.4 %bitcast_dynamic-update-slice_fusion.4 = f32[2,8,256,8,64]{2,4,3,1,0:T(8,128)} fusion(f32[2,8,256,8,64]{2,4,3,1,0:T(8,128)} %get-tuple-element.241, s32[]{:T(128)} %get-tuple-element.240, f32[8,256,8]{1,2,0:T(8,128)S(1)} %bitcast.182, f32[8,256,256]{2,1,0:T(8,128)S(1)} %fusion.77, f32[8,256,8]{1,2,0:T(8,128)S(1)} %bitcast.183, ...), kind=kOutput, calls=%fused_computation.9.clone.1 | convolution fusion | flops 562036736 | bytes 8651264 | tf_op jit(solution)/shard_map/while/body/eval_jaxpr/ktuh,kuhp->kthp/dot_general | solution.py:54
  366.7 3.7 bitcast_dynamic-update-slice_fusion.5
  370.4 3.4 bitcast_convert_fusion.1
  373.8 8.1 %copy.158 = f32[8,512,1,512]{1,0,3,2:T(8,128)} copy(f32[8,512,1,512]{1,3,0,2:T(8,128)S(1)} %bitcast_convert_fusion.1) | data formatting | bytes 16777216 | tf_op jit(solution)/shard_map/convert_element_type | solution.py:91
  381.8 9.5 %reshape.194 = f32[16,256,8,64]{1,0,3,2:T(8,128)} reshape(f32[8,512,1,512]{1,0,3,2:T(8,128)} %copy.158) | data formatting | bytes 16777216 | tf_op jit(solution)/shard_map/convert_element_type | solution.py:91
  391.3 10.2 %fusion.36 = f32[16,8,64,128]{3,0,2,1:T(8,128)} fusion(f32[16,8,64,128]{3,2,1,0:T(8,128)} %bitcast.186, f32[16,8]{0,1:T(8,128)S(1)} %copy.153, f32[16,8]{0,1:T(8,128)S(1)} %fusion.62, pred[16,16]{1,0:T(8,128)(4,1)S(1)} %iota_compare_fusion.1), kind=kOutput, calls=%fused_computation.55 | convolution fusion | flops 201332736 | bytes 8389888 | tf_op jit(solution)/shard_map/kjh,jhpn->khpn/dot_general | solution.py:86
  401.6 15.8 %fusion.29 = bf16[16,256,8,64]{1,3,2,0:T(8,128)(2,1)} fusion(f32[2,8,256,8,64]{2,4,3,1,0:T(8,128)} %get-tuple-element.56, f32[16,256,8,64]{1,0,3,2:T(8,128)S(1)} %copy-done.4, f32[8]{0:T(128)S(1)} %copy-done.9, f32[16,256,8]{1,2,0:T(8,128)S(1)} %copy.157, bf16[16,256,128,1]{2,1,3,0:T(8,128)(2,1)} %bitcast.34, f32[16,8,64,128]{3,0,2,1:T(8,128)} %fusion.36), kind=kOutput, calls=%fused_computation.46 | convolution fusion | flops 3231711232 | bytes 26345504 | tf_op jit(solution)/shard_map/khpn,ktn->kthp/dot_general | solution.py:88
  417.4 6.7 %copy.160 = bf16[16,256,8,64]{1,0,3,2:T(8,128)(2,1)} copy(bf16[16,256,8,64]{1,3,2,0:T(8,128)(2,1)} %fusion.29) | data formatting | bytes 8388608 | tf_op jit(solution)/shard_map/convert_element_type | solution.py:142
  424.1 7.1 %convert_element_type.101 = bf16[8,512,512]{1,0,2:T(8,128)(2,1)} reshape(bf16[16,256,8,64]{1,0,3,2:T(8,128)(2,1)} %copy.160) | data formatting | bytes 8388608 | tf_op jit(solution)/shard_map/convert_element_type | solution.py:142
  431.2 3.6 copy.161
  434.8 97.4 %all_to_all.64 = bf16[8,512,512]{1,2,0:T(8,128)(2,1)S(1)} all-to-all(bf16[8,512,512]{1,2,0:T(8,128)(2,1)S(1)} %copy.161), channel_id=1, replica_groups=mesh['dp'=4,'ctx'=8] {'ctx'}, dimensions={0} | all-to-all | bytes 8388608 | tf_op jit(solution)/shard_map/all_to_all | solution.py:143
  532.2 2.0 copy-done.3
  534.2 0.8 multiply_reduce_fusion
  535.1 3.3 convert_element_type.116
  538.5 2.4 fusion.27
  540.9 6.3 %copy.163 = bf16[1,512,4096]{2,1,0:T(8,128)(2,1)} copy(bf16[1,512,4096]{1,2,0:T(8,128)(2,1)} %fusion.27) | data formatting | bytes 8388608 | tf_op jit(solution)/shard_map/convert_element_type | solution.py:168
  (72 shorter events, 7.0 us)
Async XLA Ops:
  6.5 1.6 copy-start
  6.5 136.7 %all-gather.2.cloned.1.call-start = ((), (), s32[]{:S(2)}) async-start(), calls=%async_computation.5 | async-start | bytes 26214400 | tf_op jit(solution)/shard_map/all_gather | solution.py:160
  10.5 166.6 %all-to-all-start.1 = ((bf16[512,8,8]{0,2,1:T(8,128)(2,1)}), bf16[512,8,8]{0,2,1:T(8,128)(2,1)S(1)}, u32[]{:S(2)}, u32[]{:S(2)}) async-start(bf16[512,8,8]{0,2,1:T(8,128)(2,1)} %fusion.45), calls=%async_computation.1 | async-start | bytes 131072 | tf_op jit(solution)/shard_map/all_to_all | solution.py:128
  17.8 144.0 %copy-start.6 = (f32[4,5120]{1,0:T(4,128)S(1)}, f32[4,5120]{1,0:T(4,128)}, u32[]{:S(2)}) copy-start(f32[4,5120]{1,0:T(4,128)} %param.17) | copy-start | bytes 245764
  158.4 6.6 %copy-start.7 = (f32[5120]{0:T(1024)S(1)}, f32[5120]{0:T(1024)}, u32[]{:S(2)}) copy-start(f32[5120]{0:T(1024)} %param.18) | copy-start | bytes 61444
  158.4 5.0 collective-permute-start
  171.8 2.3 copy-start.5
  177.0 31.7 %all-to-all-start.2 = ((bf16[512,8,128]{2,0,1:T(8,128)(2,1)}), bf16[512,8,128]{2,0,1:T(8,128)(2,1)}, u32[]{:S(2)}, u32[]{:S(2)}) async-start(bf16[512,8,128]{2,0,1:T(8,128)(2,1)} %get-tuple-element.173), calls=%async_computation.2 | async-start | bytes 2097152 | tf_op jit(solution)/shard_map/all_to_all | solution.py:127
  188.1 25.3 %copy-start.10 = (f32[64]{0:T(128)S(1)}, f32[64]{0:T(128)}, u32[]{:S(2)}) copy-start(f32[64]{0:T(128)} %param.14) | copy-start | bytes 772
  188.1 25.4 %copy-start.11 = (f32[64]{0:T(128)S(1)}, f32[64]{0:T(128)}, u32[]{:S(2)}) copy-start(f32[64]{0:T(128)} %param.15) | copy-start | bytes 772
  188.1 25.4 %copy-start.12 = (f32[64]{0:T(128)S(1)}, f32[64]{0:T(128)}, u32[]{:S(2)}) copy-start(f32[64]{0:T(128)} %param.16) | copy-start | bytes 772
  208.8 96.8 %all-to-all-start = ((bf16[512,8,512]{0,2,1:T(8,128)(2,1)}), bf16[512,8,512]{0,2,1:T(8,128)(2,1)}, u32[]{:S(2)}, u32[]{:S(2)}) async-start(bf16[512,8,512]{0,2,1:T(8,128)(2,1)} %bitcast.180), calls=%async_computation | async-start | bytes 8388608 | tf_op jit(solution)/shard_map/all_to_all | solution.py:125
  305.6 30.3 %all-to-all-start.3 = ((bf16[512,8,128]{2,0,1:T(8,128)(2,1)}), bf16[512,8,128]{2,0,1:T(8,128)(2,1)}, u32[]{:S(2)}, u32[]{:S(2)}) async-start(bf16[512,8,128]{2,0,1:T(8,128)(2,1)} %get-tuple-element.172), calls=%async_computation.3 | async-start | bytes 2097152 | tf_op jit(solution)/shard_map/all_to_all | solution.py:126
  339.3 1.3 copy-start.2
  356.5 1.3 copy-start.2
  391.3 10.3 %copy-start.4 = (f32[16,256,8,64]{1,0,3,2:T(8,128)S(1)}, f32[16,256,8,64]{1,0,3,2:T(8,128)}, u32[]{:S(2)}) copy-start(f32[16,256,8,64]{1,0,3,2:T(8,128)} %reshape.194) | copy-start | bytes 25165828
  391.3 10.3 %copy-start.9 = (f32[8]{0:T(128)S(1)}, f32[8]{0:T(128)}, u32[]{:S(2)}) copy-start(f32[8]{0:T(128)} %dynamic_slice.29) | copy-start | bytes 100
  532.2 2.0 copy-start.3
  534.2 4.3 copy-start.8
  538.5 8.8 %copy-start.1 = (bf16[1,512,2048]{2,1,0:T(8,128)(2,1)S(1)}, bf16[1,512,2048]{2,1,0:T(8,128)(2,1)}, u32[]{:S(2)}) copy-start(bf16[1,512,2048]{2,1,0:T(8,128)(2,1)} %param.11) | copy-start | bytes 6291460
Sparse Core Ops, SparseCore 0:
  8.9 134.2 all-gather.1
where the time goes:
time: 563 us; the launch traced here: 554 us
  waiting for transfers between devices  234 us (42%)
  blocking collectives  97.4 us (17%)
  local copies, waits for them, and re-layouts  84.9 us (15%)
  matrix products  69.2 us (12%)
  other arithmetic  28.3 us (5%)
  starting transfers between devices  26.3 us (5%)
  between operations  14 us (2%)
    all_gather x1, waiting for transfers between devices, per_device(): lax.all_gather(in_weight, 'dp', axis=1, tiled=True)  125 us
    all_to_all x1, blocking collectives, head_layout(): lax.all_to_all(mixed_rows, 'ctx', split_axis=0, concat_axis=1, tiled=True)  97.4 us
    all_to_all x1, waiting for transfers between devices, head_layout(): lax.all_to_all(value_parts, 'ctx', split_axis=1, concat_axis=0, tiled=True)  91.4 us
    convert_element_type x2, local copies, waits for them, and re-layouts, ssd_group(): value_rows.astype(jnp.float32)  17.6 us
    convert_element_type x3, local copies, waits for them, and re-layouts, head_layout(): mixed_rows = pieces.reshape(full_length, local_width).astype(jnp.bfloat16)  17.4 us
    dot_general x1, matrix products, ssd_group(): jnp.einsum('khpn,ktn->kthp', entering, output_rows.astype(jnp.float32), p...  15.8 us
    dot_general x1, matrix products, per_device(): jnp.dot(token_rows, lax.all_gather(in_weight, 'dp', axis=1, tiled=True),...  15.2 us
    dot_general x2, matrix products, local_block(): jnp.einsum('ktuh,kuhp->kthp', weights, value_block, preferred_element_typ...  14.9 us
  transfers between devices with their start and end apart: 6, of which 5 were waited for; matrix products, arithmetic and copies ran while one was open for 12% of the time, Pallas kernels for 0%

commit v1 on v0

--- a/solution.py
+++ b/solution.py
@@ -157,7 +157,7 @@
     token_rows = tokens[0]
     projected = jnp.dot(
         token_rows,
-        lax.all_gather(in_weight, "dp", axis=1, tiled=True),
+        jnp.concatenate(lax.all_gather(in_weight, "dp"), axis=1),
         preferred_element_type=jnp.float32,
     ).astype(jnp.bfloat16)
     step_raw = jnp.dot(token_rows, step_weight, preferred_element_type=jnp.float32).astype(

time: 563 us -> 584 us (1.037)
  local copies, waits for them, and re-layouts: 84.9 us -> 111 us
  waiting for transfers between devices: 234 us -> 224 us
    reshape x0 -> x1, local copies, waits for them, and re-layouts: none -> 27.2 us  [per_device(): jnp.concatenate(lax.all_gather(in_weight, 'dp'), axis=1)]
    all_to_all x1, waiting for transfers between devices: 14.2 us -> 0.01 us  [head_layout(): lax.all_to_all(map_parts[:, 1], 'ctx', split_axis=1, concat_axis=0, tiled...]
    all_to_all x1, waiting for transfers between devices: 0.86 us -> 14.1 us  [head_layout(): lax.all_to_all(map_parts[:, 0], 'ctx', split_axis=1, concat_axis=0, tiled...]
    all_to_all x1, waiting for transfers between devices: 91.4 us -> 82.4 us  [head_layout(): lax.all_to_all(value_parts, 'ctx', split_axis=1, concat_axis=0, tiled=True)]
  transfers between devices with their start and end apart: 6 -> 6, of which waited for: 5 -> 4; matrix products, arithmetic and copies ran while one was open for 12% -> 21% of each run, Pallas kernels for 0% -> 0%
where the time goes in v1:
time: 584 us; the launch traced here: 574 us
  waiting for transfers between devices  224 us (38%)
  local copies, waits for them, and re-layouts  111 us (19%)
  blocking collectives  98.3 us (17%)
  matrix products  69.6 us (12%)
  other arithmetic  30.7 us (5%)
  starting transfers between devices  26 us (4%)
  between operations  14.1 us (2%)
    all_gather x1, waiting for transfers between devices, per_device(): lax.all_gather(in_weight, 'dp')  125 us
    all_to_all x1, blocking collectives, head_layout(): lax.all_to_all(mixed_rows, 'ctx', split_axis=0, concat_axis=1, tiled=True)  98.3 us
    all_to_all x1, waiting for transfers between devices, head_layout(): lax.all_to_all(value_parts, 'ctx', split_axis=1, concat_axis=0, tiled=True)  82.4 us
    reshape x1, local copies, waits for them, and re-layouts, per_device(): jnp.concatenate(lax.all_gather(in_weight, 'dp'), axis=1)  27.2 us
    convert_element_type x2, local copies, waits for them, and re-layouts, ssd_group(): value_rows.astype(jnp.float32)  17.4 us
    convert_element_type x3, local copies, waits for them, and re-layouts, head_layout(): mixed_rows = pieces.reshape(full_length, local_width).astype(jnp.bfloat16)  17.4 us
    dot_general x1, matrix products, per_device(): jnp.dot(token_rows, jnp.concatenate(lax.all_gather(in_weight, 'dp'), axis...  16.8 us
    dot_general x1, matrix products, ssd_group(): jnp.einsum('khpn,ktn->kthp', entering, output_rows.astype(jnp.float32), p...  15.9 us
  transfers between devices with their start and end apart: 6, of which 4 were waited for; matrix products, arithmetic and copies ran while one was open for 21% of the time, Pallas kernels for 0%

profile of v1, /device:TPU:0, one launch (start us, length us, event | category | flops | bytes accessed | tf_op | source)
XLA Modules:
  0.0 574.0 jit_solution(10332112448981647271)
XLA Ops:
  7.3 0.9 copy-done
  8.1 2.3 fusion.45
  10.5 7.3 %all-to-all-start.1 = ((bf16[512,8,8]{0,2,1:T(8,128)(2,1)}), bf16[512,8,8]{0,2,1:T(8,128)(2,1)S(1)}, u32[]{:S(2)}, u32[]{:S(2)}) async-start(bf16[512,8,8]{0,2,1:T(8,128)(2,1)} %fusion.45), calls=%async_computation.1 | async-start | bytes 131072 | tf_op jit(solution)/shard_map/all_to_all | solution.py:128
  17.8 125.5 %all-gather.3.cloned.1.call-done = bf16[8192,1280]{1,0:T(8,128)(2,1)} async-done(((bf16[2048,1280]{1,0:T(8,128)(2,1)}), bf16[8192,1280]{1,0:T(8,128)(2,1)}) %all-gather.3.cloned.1.call-update) | async-done | bytes 20971536 | tf_op jit(solution)/shard_map/all_gather | solution.py:160
  143.2 27.2 %copy.146 = bf16[2048,4,1280]{0,2,1:T(8,128)(2,1)} copy(bf16[2048,4,1280]{2,0,1:T(8,128)(2,1)} %bitcast.184) | data formatting | bytes 41943040 | tf_op jit(solution)/shard_map/reshape | solution.py:160
  170.4 16.8 %convolution_convert_fusion = bf16[512,5120]{1,0:T(8,128)(2,1)} fusion(bf16[2048,5120]{0,1:T(8,128)(2,1)} %bitcast.185, bf16[1,512,2048]{2,1,0:T(8,128)(2,1)S(1)} %copy-done), kind=kOutput, calls=%fused_computation.49 | convolution fusion | flops 10740039680 | bytes 28311552 | tf_op jit(solution)/shard_map/dot_general | solution.py:158
  187.2 0.9 slice.70
  188.1 3.4 collective-permute-start
  191.6 1.6 collective-permute-done
  193.1 4.0 maximum_convert_fusion
  197.2 6.7 %multiply_convert_fusion.8 = bf16[512,5120]{1,0:T(8,128)(2,1)S(1)} fusion(f32[515,5120]{1,0:T(8,128)S(1)} %maximum_convert_fusion, f32[5120]{0:T(1024)S(1)} %bitcast.198, f32[5120]{0:T(1024)S(1)} %bitcast.199, f32[5120]{0:T(1024)S(1)} %bitcast.197, f32[5120]{0:T(1024)S(1)} %bitcast.196, f32[5120]{0:T(1024)S(1)} %copy-done.8), kind=kLoop, calls=%fused_computation.40 | loop fusion | flops 34078720 | bytes 47288320 | tf_op jit(solution)/shard_map/convert_element_type | solution.py:106
  203.9 2.3 copy-done.4
  206.3 0.8 reshape.196
  207.6 1.5 slice_bitcast_fusion.1
  209.1 6.4 %all-to-all-start.3 = ((bf16[512,8,128]{2,0,1:T(8,128)(2,1)}), bf16[512,8,128]{2,0,1:T(8,128)(2,1)}, u32[]{:S(2)}, u32[]{:S(2)}) async-start(bf16[512,8,128]{2,0,1:T(8,128)(2,1)} %get-tuple-element.172), calls=%async_computation.3 | async-start | bytes 2097152 | tf_op jit(solution)/shard_map/all_to_all | solution.py:126
  215.5 4.7 slice.75
  220.2 6.5 %copy.172 = bf16[512,4096]{0,1:T(8,128)(2,1)} copy(bf16[512,4096]{1,0:T(8,128)(2,1)} %slice.75) | data formatting | bytes 8388608 | tf_op jit(solution)/shard_map/reshape | solution.py:120
  226.7 14.1 %all-to-all-done.3 = bf16[512,8,128]{2,0,1:T(8,128)(2,1)} async-done(((bf16[512,8,128]{2,0,1:T(8,128)(2,1)}), bf16[512,8,128]{2,0,1:T(8,128)(2,1)}, u32[]{:S(2)}, u32[]{:S(2)}) %all-to-all-start.3) | async-done | bytes 1048608 | tf_op jit(solution)/shard_map/all_to_all | solution.py:126
  240.8 4.5 all-to-all-start
  245.8 9.0 %reduce-window.6 = f32[16,8,2,128]{3,1,2,0:T(8,128)S(1)} reduce-window(f32[16,8,2,128]{3,1,2,0:T(8,128)S(1)} %fusion.50, f32[]{:T(128)} %constant.30.clone.1), window={size=1x1x1x128 pad=0_0x0_0x0_0x127_0}, to_apply=%region_0.1 | reduce-window | flops 4161536 | bytes 262148 | tf_op jit(solution)/shard_map/reduce-window
  255.3 82.4 %all-to-all-done = bf16[512,8,512]{0,2,1:T(8,128)(2,1)} async-done(((bf16[512,8,512]{0,2,1:T(8,128)(2,1)}), bf16[512,8,512]{0,2,1:T(8,128)(2,1)}, u32[]{:S(2)}, u32[]{:S(2)}) %all-to-all-start) | async-done | bytes 4194336 | tf_op jit(solution)/shard_map/all_to_all | solution.py:125
  337.7 4.4 all-to-all-start.2
  343.0 1.0 copy.162
  344.2 6.5 %copy.148 = bf16[8,512,1,512]{1,0,3,2:T(8,128)(2,1)} copy(bf16[8,512,1,512]{1,3,0,2:T(8,128)(2,1)} %bitcast.10) | data formatting | bytes 8388608 | tf_op jit(solution)/shard_map/all_to_all | solution.py:125
  350.7 7.1 %reshape_reshape_reshape_reshape.3 = bf16[2,8,256,8,64]{2,1,0,4,3:T(8,128)(2,1)} reshape(bf16[8,512,1,512]{1,0,3,2:T(8,128)(2,1)} %copy.148) | data formatting | bytes 8388608 | tf_op jit(solution)/shard_map/reshape;reshape;reshape;reshape | solution.py:65
  357.8 3.4 bitcast_convert_fusion.1
  361.2 8.1 %copy.163 = f32[8,512,1,512]{1,0,3,2:T(8,128)} copy(f32[8,512,1,512]{1,3,0,2:T(8,128)S(1)} %bitcast_convert_fusion.1) | data formatting | bytes 16777216 | tf_op jit(solution)/shard_map/convert_element_type | solution.py:91
  369.3 9.3 %reshape.202 = f32[16,256,8,64]{1,0,3,2:T(8,128)} reshape(f32[8,512,1,512]{1,0,3,2:T(8,128)} %copy.163) | data formatting | bytes 16777216 | tf_op jit(solution)/shard_map/convert_element_type | solution.py:91
  378.6 31.3 %while.14 = (s32[]{:T(128)}, f32[2,8,256,8,64]{2,4,3,1,0:T(8,128)}, f32[2,8,8,64,128]{4,3,2,1,0:T(8,128)}, bf16[2,8,256,8,64]{2,1,0,4,3:T(8,128)(2,1)}, f32[2,8,...) while((s32[]{:T(128)}, f32[2,8,256,8,64]{2,4,3,1,0:T(8,128)}, ...), condition=%wide.region_3.4_spmd.clone.clone, body=%wide.region_2.3_spmd.clone.clone.sunk | while | flops 967933952 | bytes 22743976 | solution.py:67
  380.2 1.7 constant_dynamic-slice_fusion.6
  382.0 1.6 fusion.77
  383.6 3.1 bitcast_dynamic-update-slice_fusion.5
  386.7 7.5 %bitcast_dynamic-update-slice_fusion.4 = f32[2,8,256,8,64]{2,4,3,1,0:T(8,128)} fusion(f32[2,8,256,8,64]{2,4,3,1,0:T(8,128)} %get-tuple-element.241, s32[]{:T(128)S(6)} %copy.213, f32[8,256,8]{1,2,0:T(8,128)S(1)} %bitcast.188, f32[8,256,256]{2,1,0:T(8,128)S(1)} %fusion.77, f32[8,256,8]{1,2,0:T(8,128)S(1)} %bitcast.189, ...), kind=kOutput, calls=%fused_computation.9.clone.1 | convolution fusion | flops 562036736 | bytes 8650756 | tf_op jit(solution)/shard_map/while/body/eval_jaxpr/ktuh,kuhp->kthp/dot_general | solution.py:54
  395.7 1.7 constant_dynamic-slice_fusion.6
  397.5 1.6 fusion.77
  399.1 3.1 bitcast_dynamic-update-slice_fusion.5
  402.2 7.5 %bitcast_dynamic-update-slice_fusion.4 = f32[2,8,256,8,64]{2,4,3,1,0:T(8,128)} fusion(f32[2,8,256,8,64]{2,4,3,1,0:T(8,128)} %get-tuple-element.241, s32[]{:T(128)S(6)} %copy.213, f32[8,256,8]{1,2,0:T(8,128)S(1)} %bitcast.188, f32[8,256,256]{2,1,0:T(8,128)S(1)} %fusion.77, f32[8,256,8]{1,2,0:T(8,128)S(1)} %bitcast.189, ...), kind=kOutput, calls=%fused_computation.9.clone.1 | convolution fusion | flops 562036736 | bytes 8650756 | tf_op jit(solution)/shard_map/while/body/eval_jaxpr/ktuh,kuhp->kthp/dot_general | solution.py:54
  409.9 10.2 %fusion.36 = f32[16,8,64,128]{3,0,2,1:T(8,128)} fusion(f32[16,8,64,128]{3,2,1,0:T(8,128)} %bitcast.192, f32[16,8]{0,1:T(8,128)S(1)} %copy.158, f32[16,8]{0,1:T(8,128)S(1)} %fusion.62, pred[16,16]{1,0:T(8,128)(4,1)S(1)} %iota_compare_fusion.1), kind=kOutput, calls=%fused_computation.55 | convolution fusion | flops 201332736 | bytes 8389888 | tf_op jit(solution)/shard_map/kjh,jhpn->khpn/dot_general | solution.py:86
  420.2 15.9 %fusion.29 = bf16[16,256,8,64]{1,3,2,0:T(8,128)(2,1)} fusion(f32[2,8,256,8,64]{2,4,3,1,0:T(8,128)} %get-tuple-element.56, f32[16,256,8,64]{1,0,3,2:T(8,128)S(1)} %copy-done.3, f32[8]{0:T(128)S(1)} %dynamic_slice.29, f32[16,256,8]{1,2,0:T(8,128)} %copy.162, bf16[16,256,128,1]{2,1,3,0:T(8,128)(2,1)} %bitcast.37, f32[16,8,64,128]{3,0,2,1:T(8,128)} %fusion.36), kind=kOutput, calls=%fused_computation.46 | convolution fusion | flops 3231711232 | bytes 26345504 | tf_op jit(solution)/shard_map/khpn,ktn->kthp/dot_general | solution.py:88
  436.0 6.7 %copy.165 = bf16[16,256,8,64]{1,0,3,2:T(8,128)(2,1)} copy(bf16[16,256,8,64]{1,3,2,0:T(8,128)(2,1)} %fusion.29) | data formatting | bytes 8388608 | tf_op jit(solution)/shard_map/convert_element_type | solution.py:142
  442.7 7.1 %convert_element_type.101 = bf16[8,512,512]{1,0,2:T(8,128)(2,1)} reshape(bf16[16,256,8,64]{1,0,3,2:T(8,128)(2,1)} %copy.165) | data formatting | bytes 8388608 | tf_op jit(solution)/shard_map/convert_element_type | solution.py:142
  449.8 3.6 copy.166
  453.4 98.3 %all_to_all.64 = bf16[8,512,512]{1,2,0:T(8,128)(2,1)S(1)} all-to-all(bf16[8,512,512]{1,2,0:T(8,128)(2,1)S(1)} %copy.166), channel_id=1, replica_groups=mesh['dp'=4,'ctx'=8] {'ctx'}, dimensions={0} | all-to-all | bytes 8388608 | tf_op jit(solution)/shard_map/all_to_all | solution.py:143
  551.7 2.0 copy-done.2
  553.7 0.8 multiply_reduce_fusion
  554.6 3.3 convert_element_type.116
  558.0 2.4 fusion.27
  560.4 6.3 %copy.168 = bf16[1,512,4096]{2,1,0:T(8,128)(2,1)} copy(bf16[1,512,4096]{1,2,0:T(8,128)(2,1)} %fusion.27) | data formatting | bytes 8388608 | tf_op jit(solution)/shard_map/convert_element_type | solution.py:168
  (75 shorter events, 6.5 us)
Async XLA Ops:
  6.5 1.6 copy-start
  6.5 136.7 %all-gather.3.cloned.1.call-start = ((), (), s32[]{:S(2)}) async-start(), calls=%async_computation.5 | async-start | bytes 26214400 | tf_op jit(solution)/shard_map/all_gather | solution.py:160
  10.5 198.6 %all-to-all-start.1 = ((bf16[512,8,8]{0,2,1:T(8,128)(2,1)}), bf16[512,8,8]{0,2,1:T(8,128)(2,1)S(1)}, u32[]{:S(2)}, u32[]{:S(2)}) async-start(bf16[512,8,8]{0,2,1:T(8,128)(2,1)} %fusion.45), calls=%async_computation.1 | async-start | bytes 131072 | tf_op jit(solution)/shard_map/all_to_all | solution.py:128
  170.4 21.1 %copy-start.7 = (f32[4,5120]{1,0:T(4,128)S(1)}, f32[4,5120]{1,0:T(4,128)}, u32[]{:S(2)}) copy-start(f32[4,5120]{1,0:T(4,128)} %param.17) | copy-start | bytes 245764
  187.2 10.0 %copy-start.8 = (f32[5120]{0:T(1024)S(1)}, f32[5120]{0:T(1024)}, u32[]{:S(2)}) copy-start(f32[5120]{0:T(1024)} %param.18) | copy-start | bytes 61444
  188.1 5.0 collective-permute-start
  203.9 2.3 copy-start.4
  209.1 31.7 %all-to-all-start.3 = ((bf16[512,8,128]{2,0,1:T(8,128)(2,1)}), bf16[512,8,128]{2,0,1:T(8,128)(2,1)}, u32[]{:S(2)}, u32[]{:S(2)}) async-start(bf16[512,8,128]{2,0,1:T(8,128)(2,1)} %get-tuple-element.172), calls=%async_computation.3 | async-start | bytes 2097152 | tf_op jit(solution)/shard_map/all_to_all | solution.py:126
  220.2 25.2 %copy-start.10 = (f32[64]{0:T(128)S(1)}, f32[64]{0:T(128)}, u32[]{:S(2)}) copy-start(f32[64]{0:T(128)} %param.14) | copy-start | bytes 772
  220.2 25.3 %copy-start.11 = (f32[64]{0:T(128)S(1)}, f32[64]{0:T(128)}, u32[]{:S(2)}) copy-start(f32[64]{0:T(128)} %param.15) | copy-start | bytes 772
  220.2 25.4 %copy-start.12 = (f32[64]{0:T(128)S(1)}, f32[64]{0:T(128)}, u32[]{:S(2)}) copy-start(f32[64]{0:T(128)} %param.16) | copy-start | bytes 772
  240.8 96.8 %all-to-all-start = ((bf16[512,8,512]{0,2,1:T(8,128)(2,1)}), bf16[512,8,512]{0,2,1:T(8,128)(2,1)}, u32[]{:S(2)}, u32[]{:S(2)}) async-start(bf16[512,8,512]{0,2,1:T(8,128)(2,1)} %bitcast.186), calls=%async_computation | async-start | bytes 8388608 | tf_op jit(solution)/shard_map/all_to_all | solution.py:125
  337.7 41.0 %all-to-all-start.2 = ((bf16[512,8,128]{2,0,1:T(8,128)(2,1)}), bf16[512,8,128]{2,0,1:T(8,128)(2,1)}, u32[]{:S(2)}, u32[]{:S(2)}) async-start(bf16[512,8,128]{2,0,1:T(8,128)(2,1)} %get-tuple-element.173), calls=%async_computation.2 | async-start | bytes 2097152 | tf_op jit(solution)/shard_map/all_to_all | solution.py:127
  378.6 0.7 copy-start.5
  386.7 7.5 %copy-start.6 = (f32[2,8,256,8]{2,3,1,0:T(8,128)S(1)}, f32[2,8,256,8]{2,3,1,0:T(8,128)}, u32[]{:S(2)}) copy-start(f32[2,8,256,8]{2,3,1,0:T(8,128)} %copy-done.5) | copy-start | bytes 393220 | tf_op jit(solution)/shard_map/while
  394.2 0.6 copy-start.5
  402.2 7.5 %copy-start.6 = (f32[2,8,256,8]{2,3,1,0:T(8,128)S(1)}, f32[2,8,256,8]{2,3,1,0:T(8,128)}, u32[]{:S(2)}) copy-start(f32[2,8,256,8]{2,3,1,0:T(8,128)} %copy-done.5) | copy-start | bytes 393220 | tf_op jit(solution)/shard_map/while
  409.9 10.3 %copy-start.3 = (f32[16,256,8,64]{1,0,3,2:T(8,128)S(1)}, f32[16,256,8,64]{1,0,3,2:T(8,128)}, u32[]{:S(2)}) copy-start(f32[16,256,8,64]{1,0,3,2:T(8,128)} %reshape.202) | copy-start | bytes 25165828
  551.7 2.0 copy-start.2
  553.7 4.3 copy-start.9
  557.9 8.8 %copy-start.1 = (bf16[1,512,2048]{2,1,0:T(8,128)(2,1)S(1)}, bf16[1,512,2048]{2,1,0:T(8,128)(2,1)}, u32[]{:S(2)}) copy-start(bf16[1,512,2048]{2,1,0:T(8,128)(2,1)} %param.11) | copy-start | bytes 6291460
Sparse Core Ops, SparseCore 0:
  8.9 134.2 all-gather.2
